TPU v7x, 256 devices: a whole 4x4x8 slice. The times are simulated.
256 devices in a mesh: cells: 64 (over x, z_lo, y), genes: 4 (over z_hi, core).
Axes of the slice: x: 4, y: 4, z: 8 (z_hi: 2, z_lo: 4; z = z_hi * 4 + z_lo), core: 2. Of those that a mesh axis runs over, the one named last changes fastest.
Arguments:
- counts: int32 [65536, 4096], P('cells', 'genes'), may hold values from 0 to 26, as said below
- library: int32 [65536], P('cells'), may hold values from 2000 to 19999
Outputs:
- adjacency: float32 [4096, 4096], P('cells', 'genes')
- connectivity: float32 [4096], P('cells')
Inputs may be any that keep to these rules, and one draw needn't show every extreme that they name: Non-negative integer counts.
All inputs are finite; a program needn't handle non-finite values.
Results may differ from a plain program's by a relative error of at most 0.006.
Values may be sent and summed in bfloat16 or wider, within the bound.
A program may use at most 128 MiB of HBM per device.

v0:
```python
import jax
import jax.numpy as jnp
from jax import lax
from jax.sharding import Mesh
from jax.sharding import PartitionSpec as P

CELLS = ("cells_0", "cells_1", "cells_2")


def from_everyone(x, axis):
    copies = jnp.broadcast_to(x, (lax.axis_size(axis), *x.shape))
    return lax.all_to_all(copies, axis, split_axis=0, concat_axis=0, tiled=True)


def of_everyone(x, axis):
    return from_everyone(x, axis).sum(axis=0)


def packed_total(arrays, axis):
    ends = [0]
    for a in arrays:
        ends.append(ends[-1] + a.size)
    total = of_everyone(jnp.concatenate([a.ravel() for a in arrays]), axis)
    return tuple((total[b:e].reshape(a.shape) for a, b, e in zip(arrays, ends, ends[1:])))


def turned_gather(arrays, axis, dims):
    turned = [jnp.moveaxis(a, dim, 0) for a, dim in zip(arrays, dims)]
    both = jnp.concatenate([t.reshape(len(t), -1) for t in turned], axis=1)
    out, at, outs = (lax.all_gather(both, axis, axis=0, tiled=True), 0, [])
    for t, dim in zip(turned, dims):
        section = out[:, at : at + t[0].size].reshape(-1, *t.shape[1:])
        outs.append(jnp.moveaxis(section, 0, dim))
        at += t[0].size
    return tuple(outs)


def sum_in_order(blocks, axes, sequence):
    inside = blocks.shape[1:]
    blocks = blocks.reshape(*(lax.axis_size(a) for a in axes), *inside)
    blocks = jnp.moveaxis(blocks, sequence, range(len(axes))).reshape(-1, *inside)
    for k in sequence:
        blocks = lax.psum_scatter(blocks, axes[k], scatter_dimension=0, tiled=True)
    return blocks[0]


def cut_along(x, dim, devices):
    dims = x.shape
    blocks = x.reshape(*dims[:dim], devices, dims[dim] // devices, *dims[dim + 1 :])
    return jnp.moveaxis(blocks, dim, 0)


def scatter_axes(x, axes, sequence, dim):
    devices = lax.axis_size(axes)
    return sum_in_order(cut_along(x, dim, devices), axes, sequence)


def normalize(counts, library):
    factor = 10000.0 / library.astype(jnp.float32)
    return jnp.log1p(counts.astype(jnp.float32) * factor[:, None]).astype(jnp.bfloat16)


def cross_product(left, right):
    return lax.dot_general(
        left, right, (((0,), (0,)), ((), ())), preferred_element_type=jnp.float32
    )


def shards(counts, library):
    own_block = normalize(counts, library)
    col_width = own_block.shape[1]
    cell_groups = lax.axis_size(CELLS)
    gene_total = col_width * lax.axis_size("genes")
    row_width = gene_total // cell_groups
    total_cells = float(counts.shape[0] * cell_groups)
    widened = own_block.astype(jnp.float32)
    local_sums = jnp.sum(widened, axis=0)
    local_squares = jnp.sum(widened * widened, axis=0)
    block_sums, block_squares = packed_total((local_sums, local_squares), CELLS)
    gene_sums, gene_squares = turned_gather((block_sums, block_squares), "genes", (0, 0))
    full_block = lax.all_gather(own_block, "genes", axis=1, tiled=True)
    gram_tile = scatter_axes(cross_product(full_block, own_block), CELLS, (0, 2, 1), 0)
    means = gene_sums / total_cells
    variances = gene_squares / total_cells - means * means
    scales = lax.rsqrt(variances + 1e-05)
    row_first = lax.axis_index(CELLS) * row_width
    col_first = lax.axis_index("genes") * col_width
    row_means = lax.dynamic_slice_in_dim(means, row_first, row_width, 0)
    col_means = lax.dynamic_slice_in_dim(means, col_first, col_width, 0)
    row_scales = lax.dynamic_slice_in_dim(scales, row_first, row_width, 0)
    col_scales = lax.dynamic_slice_in_dim(scales, col_first, col_width, 0)
    correlation = (
        (gram_tile / total_cells - row_means[:, None] * col_means[None, :])
        * row_scales[:, None]
        * col_scales[None, :]
    )
    powered = correlation**6
    row_index = row_first + jnp.arange(row_width, dtype=jnp.int32)[:, None]
    col_index = col_first + jnp.arange(col_width, dtype=jnp.int32)[None, :]
    adjacency = jnp.where(row_index == col_index, jnp.float32(0.0), powered)
    connectivity = of_everyone(jnp.sum(adjacency, axis=1), "genes")
    return (adjacency, connectivity)


def solution(mesh):
    finer = Mesh(
        mesh.devices.reshape(4, 4, 4, mesh.shape["genes"]),
        ("cells_0", "cells_1", "cells_2", "genes"),
    )
    in_specs = (P(CELLS, "genes"), P(CELLS))
    out_specs = (P(CELLS, "genes"), P(CELLS))
    return jax.shard_map(
        shards, mesh=finer, in_specs=in_specs, out_specs=out_specs, check_vma=False
    )
```

profile of v0, /device:TPU:1, one launch (start us, length us, event | category | flops | bytes accessed | tf_op | source)
XLA Modules:
  0.0 405.9 jit_solution(15591229205354031744)
XLA Ops:
  7.2 0.0 all-gather.2.cloned.1.call-start
  7.2 0.7 convert_divide_fusion
  7.9 5.6 %convert_reduce_fusion = (f32[1024]{0:T(1024)S(1)}, f32[1024]{0:T(1024)S(1)}, bf16[1024,1024]{1,0:T(8,128)(2,1)}) fusion(f32[1024]{0:T(1024)S(1)} %convert_divide_fusion, s32[1024,1024]{1,0:T(8,128)} %param.2), kind=kLoop, calls=%fused_computation.1 | loop fusion | flops 7337984 | bytes 6303744 | tf_op jit(solution)/shard_map/reduce_sum | solution.py:77
  13.5 0.0 all-gather.2.cloned.1.call-update
  13.6 0.0 reduce-scatter.4.cloned.1.call-start
  13.6 117.8 %all-gather.2.cloned.1.call-done = bf16[1024,4096]{1,0:T(8,128)(2,1)} async-done(((bf16[1024,1024]{1,0:T(8,128)(2,1)}), bf16[1024,4096]{1,0:T(8,128)(2,1)}) %all-gather.2.cloned.1.call-update) | async-done | bytes 8388624 | tf_op jit(solution)/shard_map/all_gather | solution.py:81
  131.4 12.0 %fusion.11 = f32[4096,1024]{1,0:T(8,128)S(1)} fusion(bf16[1024,4096]{1,0:T(8,128)(2,1)} %all-gather.2.cloned.1.call-done, bf16[1024,1024]{1,0:T(8,128)(2,1)} %get-tuple-element.6), kind=kOutput, calls=%fused_computation.27 | convolution fusion | flops 8589934592 | bytes 27262976 | tf_op jit(solution)/shard_map/dot_general | solution.py:64
  143.5 6.6 %copy.6 = f32[4,4,4,64,1024]{4,3,2,1,0:T(8,128)} copy(f32[4,4,4,64,1024]{4,3,1,2,0:T(8,128)S(1)} %bitcast.27) | data formatting | bytes 33554432 | tf_op jit(solution)/shard_map/transpose | solution.py:41
  150.0 0.0 reduce-scatter.4.cloned.1.call-update
  150.1 0.0 reduce-scatter.6.cloned.1.call-start
  150.1 146.2 %reduce-scatter.4.cloned.1.call-done = f32[16,64,1024]{2,1,0:T(8,128)} async-done(((f32[64,64,1024]{2,1,0:T(8,128)}), f32[16,64,1024]{2,1,0:T(8,128)}) %reduce-scatter.4.cloned.1.call-update) | async-done | bytes 4194320 | tf_op jit(solution)/shard_map/reduce_scatter | solution.py:43
  296.3 0.0 reduce-scatter.6.cloned.1.call-update
  296.4 1.1 broadcast_in_dim.8
  297.4 8.9 %all-to-all-start = ((f32[64,1,2048]{2,1,0:T(1,128)}), f32[64,1,2048]{2,1,0:T(1,128)S(1)}, u32[]{:S(2)}, u32[]{:S(2)}) async-start(f32[64,1,2048]{2,1,0:T(1,128)} %broadcast_in_dim.8), calls=%async_computation.3 | async-start | bytes 1048576 | tf_op jit(solution)/shard_map/all_to_all | solution.py:12
  306.3 0.0 reduce-scatter.8.cloned.1.call-start
  306.4 45.9 %reduce-scatter.6.cloned.1.call-done = f32[4,64,1024]{2,1,0:T(8,128)} async-done(((f32[16,64,1024]{2,1,0:T(8,128)}), f32[4,64,1024]{2,1,0:T(8,128)}) %reduce-scatter.6.cloned.1.call-update) | async-done | bytes 1048592 | tf_op jit(solution)/shard_map/reduce_scatter | solution.py:43
  352.3 0.0 reduce-scatter.8.cloned.1.call-update
  352.3 0.3 reduce_sum.47
  352.7 9.6 %all_gather.7 = f32[4096,2]{0,1:T(2,128)S(1)} all-gather(f32[1024,2]{0,1:T(2,128)S(1)} %pad_maximum_fusion.1), channel_id=1, replica_groups=mesh['cells_0'=4,'cells_1'=4,'cells_2'=4,'genes'=4] {'genes'}, dimensions={0}, use_global_device_ids=true | all-gather | bytes 40960 | tf_op jit(solution)/shard_map/all_gather | solution.py:30
  362.3 0.1 fusion.6
  362.4 22.1 %reduce-scatter.8.cloned.1.call-done = f32[1,64,1024]{2,1,0:T(8,128)} async-done(((f32[4,64,1024]{2,1,0:T(8,128)}), f32[1,64,1024]{2,1,0:T(8,128)}) %reduce-scatter.8.cloned.1.call-update) | async-done | bytes 262160 | tf_op jit(solution)/shard_map/reduce_scatter | solution.py:43
  384.4 1.9 fusion.8
  386.4 12.4 %all_to_all.12 = f32[4,1,64]{2,1,0:T(1,128)S(1)} all-to-all(f32[4,1,64]{2,1,0:T(1,128)S(1)} %broadcast_in_dim.10), channel_id=1, replica_groups=mesh['cells_0'=4,'cells_1'=4,'cells_2'=4,'genes'=4] {'genes'}, dimensions={0} | all-to-all | bytes 2048 | tf_op jit(solution)/shard_map/all_to_all | solution.py:12
  398.8 0.5 reduce_sum.49
  (9 shorter events, 0.1 us)
Async XLA Ops:
  7.2 124.3 %all-gather.2.cloned.1.call-start = ((), (), s32[]{:S(2)}) async-start(), calls=%async_computation.5 | async-start | bytes 10485760 | tf_op jit(solution)/shard_map/all_gather | solution.py:81
  13.6 282.8 %reduce-scatter.4.cloned.1.call-start = ((), (), s32[]{:S(2)}) async-start(), calls=%async_computation.6 | async-start | bytes 20971520 | tf_op jit(solution)/shard_map/reduce_scatter | solution.py:43
  150.1 202.2 %reduce-scatter.6.cloned.1.call-start = ((), (), s32[]{:S(2)}) async-start(), calls=%async_computation.7 | async-start | bytes 5242880 | tf_op jit(solution)/shard_map/reduce_scatter | solution.py:43
  297.4 54.9 %all-to-all-start = ((f32[64,1,2048]{2,1,0:T(1,128)}), f32[64,1,2048]{2,1,0:T(1,128)S(1)}, u32[]{:S(2)}, u32[]{:S(2)}) async-start(f32[64,1,2048]{2,1,0:T(1,128)} %broadcast_in_dim.8), calls=%async_computation.3 | async-start | bytes 1048576 | tf_op jit(solution)/shard_map/all_to_all | solution.py:12
  306.3 78.1 %reduce-scatter.8.cloned.1.call-start = ((), (), s32[]{:S(2)}) async-start(), calls=%async_computation.8 | async-start | bytes 1310720 | tf_op jit(solution)/shard_map/reduce_scatter | solution.py:43
Sparse Core Ops, SparseCore 0:
  13.7 117.6 all-gather.1
  150.2 146.0 reduce-scatter.3
  298.9 53.3 reduce-scatter.5
  354.7 29.7 reduce-scatter.7
where the time goes:
time: 406 us
  waiting for transfers between devices  332 us (82%)
  blocking collectives  22 us (5%)
  between operations  13.8 us (3%)
  matrix products  12 us (3%)
  other arithmetic  9.16 us (2%)
  starting transfers between devices  9.05 us (2%)
  local copies, waits for them, and re-layouts  7.75 us (2%)
    reduce_scatter x3, waiting for transfers between devices, sum_in_order(): blocks = lax.psum_scatter(blocks, axes[k], scatter_dimension=0, tiled=True)  214 us
    all_gather x1, waiting for transfers between devices, shards(): full_block = lax.all_gather(own_block, 'genes', axis=1, tiled=True)  118 us
    all_to_all x1, blocking collectives, from_everyone(): return lax.all_to_all(copies, axis, split_axis=0, concat_axis=0, tiled=True)  12.4 us
    dot_general x1, matrix products, cross_product(): lax.dot_general(left, right, (((0,), (0,)), ((), ())), preferred_element_...  12 us
    all_gather x1, blocking collectives, turned_gather(): out, at, outs = (lax.all_gather(both, axis, axis=0, tiled=True), 0, [])  9.55 us
    all_to_all x1, starting transfers between devices, from_everyone(): return lax.all_to_all(copies, axis, split_axis=0, concat_axis=0, tiled=True)  8.89 us
  transfers between devices with their start and end apart: 5, of which 4 were waited for; matrix products, arithmetic and copies ran while one was open for 0% of the time, Pallas kernels for 0%

commit v1 on v0

--- a/solution.py
+++ b/solution.py
@@ -78,7 +78,8 @@
     local_squares = jnp.sum(widened * widened, axis=0)
     block_sums, block_squares = packed_total((local_sums, local_squares), CELLS)
     gene_sums, gene_squares = turned_gather((block_sums, block_squares), "genes", (0, 0))
-    full_block = lax.all_gather(own_block, "genes", axis=1, tiled=True)
+    sent = jnp.stack([own_block] * lax.axis_size("genes"))
+    full_block = jnp.concatenate(lax.all_to_all(sent, "genes", 0, 0), axis=1)
     gram_tile = scatter_axes(cross_product(full_block, own_block), CELLS, (0, 2, 1), 0)
     means = gene_sums / total_cells
     variances = gene_squares / total_cells - means * means

time: 406 us -> 491 us (1.21)
  blocking collectives: 22 us -> 219 us
  waiting for transfers between devices: 332 us -> 217 us
    all_to_all x0 -> x1, blocking collectives: none -> 197 us  [shards(): full_block = jnp.concatenate(lax.all_to_all(sent, 'genes', 0, 0), axis=1)]
    all_gather x1 -> x0, waiting for transfers between devices: 118 us -> none  [shards(): full_block = lax.all_gather(own_block, 'genes', axis=1, tiled=True)]
  transfers between devices with their start and end apart: 5 -> 4, of which waited for: 4 -> 3; matrix products, arithmetic and copies ran while one was open for 0% -> 0% of each run, Pallas kernels for 0% -> 0%
where the time goes in v1:
time: 491 us
  blocking collectives  219 us (45%)
  waiting for transfers between devices  217 us (44%)
  between operations  13.9 us (3%)
  local copies, waits for them, and re-layouts  11.8 us (2%)
  matrix products  11.6 us (2%)
  other arithmetic  9.16 us (2%)
  starting transfers between devices  9 us (2%)
    reduce_scatter x3, waiting for transfers between devices, sum_in_order(): blocks = lax.psum_scatter(blocks, axes[k], scatter_dimension=0, tiled=True)  217 us
    all_to_all x1, blocking collectives, shards(): full_block = jnp.concatenate(lax.all_to_all(sent, 'genes', 0, 0), axis=1)  197 us
    all_to_all x1, blocking collectives, from_everyone(): return lax.all_to_all(copies, axis, split_axis=0, concat_axis=0, tiled=True)  12.5 us
    dot_general x1, matrix products, cross_product(): lax.dot_general(left, right, (((0,), (0,)), ((), ())), preferred_element_...  11.6 us
  transfers between devices with their start and end apart: 4, of which 3 were waited for; matrix products, arithmetic and copies ran while one was open for 0% of the time, Pallas kernels for 0%

profile of v1, /device:TPU:1, one launch (start us, length us, event | category | flops | bytes accessed | tf_op | source)
XLA Modules:
  0.0 490.8 jit_solution(13700427106023687262)
XLA Ops:
  7.2 0.0 reduce-scatter.4.cloned.1.call-start
  7.2 0.7 convert_divide_fusion
  7.9 5.6 %convert_reduce_fusion = (f32[1024]{0:T(1024)S(1)}, f32[1024]{0:T(1024)S(1)}, bf16[1024,1024]{1,0:T(8,128)(2,1)}) fusion(f32[1024]{0:T(1024)S(1)} %convert_divide_fusion, s32[1024,1024]{1,0:T(8,128)} %param.2), kind=kLoop, calls=%fused_computation.2 | loop fusion | flops 7337984 | bytes 6303744 | tf_op jit(solution)/shard_map/reduce_sum | solution.py:77
  13.5 2.9 copy.9
  16.4 1.2 stack.2
  17.6 196.6 %all_to_all.17 = bf16[4,1024,1024]{1,2,0:T(8,128)(2,1)} all-to-all(bf16[4,1024,1024]{1,2,0:T(8,128)(2,1)S(1)} %stack.2), channel_id=1, replica_groups=mesh['cells_0'=4,'cells_1'=4,'cells_2'=4,'genes'=4] {'genes'}, dimensions={0} | all-to-all | bytes 16777216 | tf_op jit(solution)/shard_map/all_to_all | solution.py:82
  214.2 11.6 %convolution_bitcast_fusion = f32[4,4,4,64,1024]{4,3,1,2,0:T(8,128)S(1)} fusion(bf16[4,4,4,64,1024]{4,3,2,1,0:T(8,128)(2,1)} %bitcast.37, bf16[1024,1024]{1,0:T(8,128)(2,1)S(1)} %copy-done), kind=kOutput, calls=%fused_computation | convolution fusion | flops 8589934592 | bytes 27262976 | tf_op jit(solution)/shard_map/dot_general | solution.py:64
  225.8 6.6 %copy.10 = f32[4,4,4,64,1024]{4,3,2,1,0:T(8,128)} copy(f32[4,4,4,64,1024]{4,3,1,2,0:T(8,128)S(1)} %convolution_bitcast_fusion) | data formatting | bytes 33554432 | tf_op jit(solution)/shard_map/transpose | solution.py:41
  232.4 0.0 reduce-scatter.4.cloned.1.call-update
  232.4 0.0 reduce-scatter.6.cloned.1.call-start
  232.4 148.6 %reduce-scatter.4.cloned.1.call-done = f32[16,64,1024]{2,1,0:T(8,128)} async-done(((f32[64,64,1024]{2,1,0:T(8,128)}), f32[16,64,1024]{2,1,0:T(8,128)}) %reduce-scatter.4.cloned.1.call-update) | async-done | bytes 4194320 | tf_op jit(solution)/shard_map/reduce_scatter | solution.py:43
  381.1 0.0 reduce-scatter.6.cloned.1.call-update
  381.1 1.1 broadcast_in_dim.8
  382.2 8.9 %all-to-all-start.1 = ((f32[64,1,2048]{2,1,0:T(1,128)}), f32[64,1,2048]{2,1,0:T(1,128)S(1)}, u32[]{:S(2)}, u32[]{:S(2)}) async-start(f32[64,1,2048]{2,1,0:T(1,128)} %broadcast_in_dim.8), calls=%async_computation.4 | async-start | bytes 1048576 | tf_op jit(solution)/shard_map/all_to_all | solution.py:12
  391.1 0.0 reduce-scatter.8.cloned.1.call-start
  391.1 45.9 %reduce-scatter.6.cloned.1.call-done = f32[4,64,1024]{2,1,0:T(8,128)} async-done(((f32[16,64,1024]{2,1,0:T(8,128)}), f32[4,64,1024]{2,1,0:T(8,128)}) %reduce-scatter.6.cloned.1.call-update) | async-done | bytes 1048592 | tf_op jit(solution)/shard_map/reduce_scatter | solution.py:43
  437.0 0.0 reduce-scatter.8.cloned.1.call-update
  437.0 0.3 reduce_sum.47
  437.4 9.6 %all_gather.3 = f32[4096,2]{0,1:T(2,128)S(1)} all-gather(f32[1024,2]{0,1:T(2,128)S(1)} %pad_maximum_fusion.1), channel_id=1, replica_groups=mesh['cells_0'=4,'cells_1'=4,'cells_2'=4,'genes'=4] {'genes'}, dimensions={0}, use_global_device_ids=true | all-gather | bytes 40960 | tf_op jit(solution)/shard_map/all_gather | solution.py:30
  447.0 0.1 fusion.7
  447.1 22.2 %reduce-scatter.8.cloned.1.call-done = f32[1,64,1024]{2,1,0:T(8,128)} async-done(((f32[4,64,1024]{2,1,0:T(8,128)}), f32[1,64,1024]{2,1,0:T(8,128)}) %reduce-scatter.8.cloned.1.call-update) | async-done | bytes 262160 | tf_op jit(solution)/shard_map/reduce_scatter | solution.py:43
  469.3 1.9 fusion.9
  471.3 12.5 %all_to_all.18 = f32[4,1,64]{2,1,0:T(1,128)S(1)} all-to-all(f32[4,1,64]{2,1,0:T(1,128)S(1)} %broadcast_in_dim.10), channel_id=1, replica_groups=mesh['cells_0'=4,'cells_1'=4,'cells_2'=4,'genes'=4] {'genes'}, dimensions={0} | all-to-all | bytes 2048 | tf_op jit(solution)/shard_map/all_to_all | solution.py:12
  483.7 0.5 reduce_sum.49
  (11 shorter events, 0.1 us)
Async XLA Ops:
  7.2 373.9 %reduce-scatter.4.cloned.1.call-start = ((), (), s32[]{:S(2)}) async-start(), calls=%async_computation.6 | async-start | bytes 20971520 | tf_op jit(solution)/shard_map/reduce_scatter | solution.py:43
  17.6 196.6 %copy-start = (bf16[1024,1024]{1,0:T(8,128)(2,1)S(1)}, bf16[1024,1024]{1,0:T(8,128)(2,1)}, u32[]{:S(2)}) copy-start(bf16[1024,1024]{1,0:T(8,128)(2,1)} %get-tuple-element.6) | copy-start | bytes 6291460
  232.4 204.6 %reduce-scatter.6.cloned.1.call-start = ((), (), s32[]{:S(2)}) async-start(), calls=%async_computation.7 | async-start | bytes 5242880 | tf_op jit(solution)/shard_map/reduce_scatter | solution.py:43
  382.2 54.9 %all-to-all-start.1 = ((f32[64,1,2048]{2,1,0:T(1,128)}), f32[64,1,2048]{2,1,0:T(1,128)S(1)}, u32[]{:S(2)}, u32[]{:S(2)}) async-start(f32[64,1,2048]{2,1,0:T(1,128)} %broadcast_in_dim.8), calls=%async_computation.4 | async-start | bytes 1048576 | tf_op jit(solution)/shard_map/all_to_all | solution.py:12
  391.1 78.3 %reduce-scatter.8.cloned.1.call-start = ((), (), s32[]{:S(2)}) async-start(), calls=%async_computation.8 | async-start | bytes 1310720 | tf_op jit(solution)/shard_map/reduce_scatter | solution.py:43
Sparse Core Ops, SparseCore 0:
  232.5 148.4 reduce-scatter.3
  383.6 53.3 reduce-scatter.5
  439.5 29.7 reduce-scatter.7
